TPU v7x, 32 devices: a whole 2x2x4 slice. The times are simulated.
32 devices in a mesh: rep: 4 (over y, core), shard: 8 (over z, x).
Axes of the slice: x: 2, y: 2, z: 4, core: 2. Of those that a mesh axis runs over, the one named last changes fastest.
Arguments:
- hidden: bfloat16 [14336, 3584], P(('rep', 'shard')), may hold values from -144 to 144
- cotangent: bfloat16 [14336, 1024], P(('rep', 'shard')), may hold values from -6 to 6
- seq_ids: int32 [32, 448], P(('rep', 'shard')), may hold values from 0 to 3, as said below
- response_mask: int32 [32, 448], P(('rep', 'shard')), may hold values from 0 to 1, as said below
- group_ids: int32 [32, 4], P(('rep', 'shard')), may hold values from 0 to 15
- rewards: float32 [32, 4], P(('rep', 'shard')), may hold values from -6 to 6
- new_logp: float32 [32, 448], P(('rep', 'shard')), may hold values from -1.5 to -0.1
- old_logp: float32 [32, 448], P(('rep', 'shard')), may hold values from -1.5 to -0.1
- ref_logp: float32 [32, 448], P(('rep', 'shard')), may hold values from -1.5 to -0.1
- master: float32 [3, 3584, 1024], P(None, 'shard'), may hold values from -6 to 6
Outputs:
- new_master: float32 [3584, 1024], P('shard')
- rollout: bfloat16 [3, 3584, 2048], P(None, None, 'shard')
Inputs may be any that keep to these rules, and one draw needn't show every extreme that they name: `seq_ids`: each row numbers its device's 4 sequences in token order, never falling, each with one token or more. `response_mask`: within a sequence, prompt tokens come before response tokens; a sequence may have no response tokens.
All inputs are finite; a program needn't handle non-finite values.
Results may differ from a plain program's by a relative error of at most 0.0095.
Values may be sent and summed in bfloat16 or wider, within the bound.
A program may use at most 128 MiB of HBM per device.

v0:
```python
import jax
import jax.numpy as jnp
from jax import lax
from jax.sharding import PartitionSpec as P

HEAD = 128
KV_HEADS = 4
TP = 8
SEQ_DEV = 4


def token_coef(seq_row, mask_row, adv_row, new_row, old_row, ref_row):
    onehot = (seq_row[:, None] == jnp.arange(SEQ_DEV, dtype=jnp.int32)[None, :]).astype(jnp.float32)
    maskf = mask_row.astype(jnp.float32)
    lengths = jnp.maximum(jnp.dot(maskf, onehot, precision=lax.Precision.HIGHEST), 1.0)
    tok_len = jnp.dot(onehot, lengths, precision=lax.Precision.HIGHEST)
    tok_adv = jnp.dot(onehot, adv_row, precision=lax.Precision.HIGHEST)
    surrogate = -tok_adv * jnp.exp(new_row - old_row) + 0.2 * (1.0 - jnp.exp(ref_row - new_row))
    return maskf / tok_len * surrogate


def group_advantage(group_flat, reward_flat, stats):
    groups = stats.shape[1]
    onehot = (group_flat[:, None] == jnp.arange(groups, dtype=jnp.int32)[None, :]).astype(
        jnp.float32
    )
    count = jnp.maximum(stats[0], 1.0)
    mean = stats[1] / count
    spread = jnp.sqrt(jnp.maximum(stats[2] / count - mean * mean, 0.0))
    tok_mean = jnp.dot(onehot, mean, precision=lax.Precision.HIGHEST)
    tok_std = jnp.dot(onehot, jnp.maximum(spread, 0.5), precision=lax.Precision.HIGHEST)
    return (reward_flat - tok_mean) / tok_std


def group_sums(group_flat, reward_flat, groups):
    onehot = (group_flat[:, None] == jnp.arange(groups, dtype=jnp.int32)[None, :]).astype(
        jnp.float32
    )
    values = jnp.stack([jnp.ones_like(reward_flat), reward_flat, reward_flat * reward_flat], axis=0)
    return jnp.dot(values, onehot, precision=lax.Precision.HIGHEST)


def rounded(term):
    return lax.optimization_barrier(term.astype(jnp.bfloat16)).astype(jnp.float32)


def rollout_blocks(weights):
    layer_count = weights.shape[0]
    row_count = weights.shape[1]
    paired = weights.reshape(layer_count, row_count, 2, KV_HEADS, HEAD).transpose(0, 1, 3, 2, 4)
    paired = paired.reshape(layer_count, row_count, KV_HEADS, 2 * HEAD)
    by_rank = jnp.repeat(paired, TP // KV_HEADS, axis=2)
    copies = jnp.tile(by_rank, (1, 1, lax.axis_size("shard") // TP, 1))
    return copies.reshape(layer_count, row_count, lax.axis_size("shard") * 2 * HEAD)


def per_device(
    hidden,
    cotangent,
    seq_ids,
    response_mask,
    group_ids,
    rewards,
    new_logp,
    old_logp,
    ref_logp,
    master,
):
    n_rep = lax.axis_size("rep")
    n_shard = lax.axis_size("shard")
    groups = n_rep * n_shard * SEQ_DEV // 8
    rest_cols = lax.all_to_all(
        rollout_blocks(master[1:].astype(jnp.bfloat16)),
        "shard",
        split_axis=2,
        concat_axis=1,
        tiled=True,
    )
    local_sums = group_sums(group_ids[0], rewards[0], groups)
    stats = lax.psum(local_sums, ("rep", "shard"))
    advantage = group_advantage(group_ids[0], rewards[0], stats)
    coef = token_coef(
        seq_ids[0], response_mask[0], advantage, new_logp[0], old_logp[0], ref_logp[0]
    )
    delta = (coef[:, None] * cotangent.astype(jnp.float32)).astype(jnp.bfloat16)
    feature_count = hidden.shape[1]
    partial_value = lax.psum_scatter(
        rounded(
            lax.dot_general(
                hidden, delta, (((0,), (0,)), ((), ())), preferred_element_type=jnp.float32
            )
        ).astype(jnp.bfloat16),
        "shard",
        scatter_dimension=0,
        tiled=True,
    )
    grad = lax.psum(partial_value, "rep").astype(jnp.float32)
    squares = lax.psum(jnp.sum(grad * grad), "shard")
    rms = jnp.sqrt(squares / (feature_count * grad.shape[1]) + 1e-06)
    new_master = master[0] - 0.5 * grad / rms
    first_cols = lax.all_to_all(
        rollout_blocks(new_master[None].astype(jnp.bfloat16)),
        "shard",
        split_axis=2,
        concat_axis=1,
        tiled=True,
    )
    rollout = jnp.concatenate([first_cols, rest_cols], axis=0)
    return (new_master, rollout)


def solution(mesh):
    in_specs = (
        P(("rep", "shard"), None),
        P(("rep", "shard"), None),
        P(("rep", "shard"), None),
        P(("rep", "shard"), None),
        P(("rep", "shard"), None),
        P(("rep", "shard"), None),
        P(("rep", "shard"), None),
        P(("rep", "shard"), None),
        P(("rep", "shard"), None),
        P(None, "shard", None),
    )
    out_specs = (P("shard", None), P(None, None, "shard"))
    return jax.shard_map(
        per_device, mesh=mesh, in_specs=in_specs, out_specs=out_specs, check_vma=False
    )
```

profile of v0, /device:TPU:0, one launch (start us, length us, event | category | flops | bytes accessed | tf_op | source)
XLA Modules:
  0.0 468.4 jit_solution(8274017862780211825)
XLA Ops:
  7.2 0.0 reduce-scatter.4.cloned.1.call-start
  7.2 0.8 mul.39
  8.1 1.0 fusion.15
  9.0 41.9 %psum.21 = f32[3,16]{1,0:T(4,128)S(1)} all-reduce(f32[3,16]{1,0:T(4,128)S(1)} %fusion.15), channel_id=1, replica_groups=mesh['rep'=4,'shard'=8] {'rep','shard'}, use_global_device_ids=true, to_apply=%region_0.0 | all-reduce | flops 48 | bytes 384 | tf_op jit(solution)/shard_map/psum | solution.py:80
  51.0 0.8 convolution_bitcast_fusion
  51.8 0.9 fusion.8
  52.7 0.7 convert_element_type.31
  53.4 0.9 fusion.5
  54.3 1.0 fusion.10
  55.3 1.0 fusion.11
  56.3 0.8 subtract_exponential_fusion
  57.1 7.5 %fusion = bf16[3584,1024]{0,1:T(8,128)(2,1)} fusion(bf16[448,3584]{1,0:T(8,128)(2,1)S(1)} %copy-done, bf16[448,1024]{1,0:T(8,128)(2,1)} %param.11, f32[448]{0:T(512)S(1)} %add_multiply_fusion), kind=kOutput, calls=%fused_computation.1 | convolution fusion | flops 3293380608 | bytes 11470592 | tf_op jit(solution)/shard_map/dot_general | solution.py:89
  64.6 10.4 %copy.47 = bf16[3584,1024]{1,0:T(8,128)(2,1)} copy(bf16[3584,1024]{0,1:T(8,128)(2,1)} %fusion) | data formatting | bytes 14680064
  75.0 0.0 reduce-scatter.4.cloned.1.call-update
  75.0 2.3 slice.36
  77.4 2.3 reshape.41
  79.6 5.7 %copy.49 = bf16[2,448,2,4,128]{1,0,4,2,3:T(2,128)(2,1)S(1)} copy(bf16[2,448,2,4,128]{4,3,2,1,0:T(4,128)(2,1)} %reshape.41) | data formatting | bytes 3670016 | tf_op jit(solution)/shard_map/transpose | solution.py:50
  85.3 4.2 broadcast_in_dim.15
  89.5 5.3 %all-to-all-start.1 = ((bf16[2,448,2048]{1,0,2:T(2,128)(2,1)}), bf16[2,448,2048]{1,0,2:T(2,128)(2,1)}, u32[]{:S(2)}, u32[]{:S(2)}) async-start(bf16[2,448,2048]{1,0,2:T(2,128)(2,1)} %bitcast.83), calls=%async_computation.1 | async-start | bytes 8388608 | tf_op jit(solution)/shard_map/all_to_all | solution.py:72
  94.8 0.0 all-reduce.2.cloned.1.call-start
  94.9 188.3 %reduce-scatter.4.cloned.1.call-done = bf16[448,1024]{1,0:T(8,128)(2,1)} async-done(((bf16[3584,1024]{1,0:T(8,128)(2,1)}), bf16[448,1024]{1,0:T(8,128)(2,1)}) %reduce-scatter.4.cloned.1.call-update) | async-done | bytes 917520
  283.2 2.2 copy.48
  285.4 0.0 all-reduce.2.cloned.1.call-update
  285.4 36.1 %all-reduce.2.cloned.1.call-done = bf16[448,1024]{0,1:T(8,128)(2,1)} async-done(((bf16[448,1024]{0,1:T(8,128)(2,1)}), bf16[448,1024]{0,1:T(8,128)(2,1)}) %all-reduce.2.cloned.1.call-update) | async-done | bytes 917520 | tf_op jit(solution)/shard_map/psum | solution.py:97
  321.5 2.4 fusion.3
  323.9 1.9 copy.51
  325.7 22.1 %psum.23 = f32[]{:T(128)} all-reduce(f32[]{:T(128)} %fusion.3), channel_id=1, replica_groups=mesh['rep'=4,'shard'=8] {'shard'}, use_global_device_ids=true, to_apply=%region_4.0 | all-reduce | flops 1 | bytes 8 | tf_op jit(solution)/shard_map/psum | solution.py:98
  348.6 3.0 fusion.36
  351.6 3.6 copy.33
  355.2 2.7 reshape.40
  357.9 0.7 copy.34
  358.6 2.5 broadcast_in_dim.6
  361.1 5.3 %broadcast_in_dim.14 = bf16[1,448,2048]{2,1,0:T(8,128)(2,1)} reshape(bf16[448,4,2,256]{3,2,1,0:T(2,128)(2,1)} %broadcast_in_dim.6) | data formatting | bytes 3670016 | tf_op jit(solution)/shard_map/broadcast_in_dim | solution.py:52
  366.4 10.7 %copy.35 = bf16[1,448,2048]{1,0,2:T(2,128)(2,1)} copy(bf16[1,448,2048]{2,1,0:T(8,128)(2,1)} %broadcast_in_dim.14) | data formatting | bytes 3670016 | tf_op jit(solution)/shard_map/broadcast_in_dim | solution.py:52
  377.1 0.5 broadcast.50
  377.6 15.4 %reduce = bf16[2048,448]{1,0:T(8,128)(2,1)} reduce(bf16[2048,1,448]{2,1,0:T(2,128)(2,1)} %bitcast.84, bf16[]{:T(256)} %broadcast.50), dimensions={1}, to_apply=%bitcast.77.reduce_sub_computation | reduce | bytes 3670018
  393.1 6.8 %reshape.57 = bf16[8,2,57344]{2,1,0:T(2,128)(2,1)} reshape(bf16[2048,448]{1,0:T(8,128)(2,1)} %reduce) | data formatting | bytes 3670016
  399.8 4.3 all-to-all-start
  404.2 11.1 %copy.46 = bf16[2,448,8,256]{3,1,2,0:T(8,128)(2,1)} copy(bf16[2,448,8,256]{1,0,3,2:T(2,128)(2,1)} %bitcast.27) | data formatting | bytes 7340032 | tf_op jit(solution)/shard_map/all_to_all | solution.py:72
  415.3 1.7 copy.42
  417.0 25.9 %all-to-all-done = bf16[8,2,57344]{2,1,0:T(2,128)(2,1)} async-done(((bf16[8,2,57344]{2,1,0:T(2,128)(2,1)}), bf16[8,2,57344]{2,1,0:T(2,128)(2,1)}, u32[]{:S(2)}, u32[]{:S(2)}) %all-to-all-start) | async-done | bytes 1835040 | tf_op jit(solution)/shard_map/all_to_all | solution.py:101
  442.9 7.2 %reshape.58 = bf16[2048,1,448]{2,1,0:T(2,128)(2,1)} reshape(bf16[8,2,57344]{2,1,0:T(2,128)(2,1)} %all-to-all-done) | data formatting | bytes 3670016
  450.1 2.8 copy.50
  452.9 3.0 copy.43
  455.8 2.0 copy.37
  457.9 0.6 copy-done.2
  458.4 2.9 pad_maximum_fusion
  461.3 0.2 copy-done.1
  (12 shorter events, 0.0 us)
Async XLA Ops:
  7.2 49.9 %copy-start = (bf16[448,3584]{1,0:T(8,128)(2,1)S(1)}, bf16[448,3584]{1,0:T(8,128)(2,1)}, u32[]{:S(2)}) copy-start(bf16[448,3584]{1,0:T(8,128)(2,1)} %param.10) | copy-start | bytes 9633796
  7.2 276.0 %reduce-scatter.4.cloned.1.call-start = ((), (), s32[]{:S(2)}) async-start(), calls=%async_computation.4 | async-start | bytes 8257536
  89.5 310.4 %all-to-all-start.1 = ((bf16[2,448,2048]{1,0,2:T(2,128)(2,1)}), bf16[2,448,2048]{1,0,2:T(2,128)(2,1)}, u32[]{:S(2)}, u32[]{:S(2)}) async-start(bf16[2,448,2048]{1,0,2:T(2,128)(2,1)} %bitcast.83), calls=%async_computation.1 | async-start | bytes 8388608 | tf_op jit(solution)/shard_map/all_to_all | solution.py:72
  94.8 226.7 %all-reduce.2.cloned.1.call-start = ((), (), s32[]{:S(2)}) async-start(), calls=%async_computation.3 | async-start | bytes 2097152 | tf_op jit(solution)/shard_map/psum | solution.py:97
  285.4 38.5 %slice-start = ((f32[3,448,1024]{2,1,0:T(8,128)}), f32[1,448,1024]{2,1,0:T(8,128)S(1)}, s32[]{:S(2)}) async-start(f32[3,448,1024]{2,1,0:T(8,128)} %param.19), calls=%async_computation.5 | async-start | bytes 3670016 | tf_op jit(solution)/shard_map/slice | solution.py:100
  323.9 24.7 %copy-start.3 = (bf16[448,1024]{0,1:T(8,128)(2,1)S(1)}, bf16[448,1024]{0,1:T(8,128)(2,1)}, u32[]{:S(2)}) copy-start(bf16[448,1024]{0,1:T(8,128)(2,1)} %all-reduce.2.cloned.1.call-done) | copy-start | bytes 2752516
  399.8 43.1 %all-to-all-start = ((bf16[8,2,57344]{2,1,0:T(2,128)(2,1)}), bf16[8,2,57344]{2,1,0:T(2,128)(2,1)}, u32[]{:S(2)}, u32[]{:S(2)}) async-start(bf16[8,2,57344]{2,1,0:T(2,128)(2,1)} %reshape.57), calls=%async_computation | async-start | bytes 3670016 | tf_op jit(solution)/shard_map/all_to_all | solution.py:101
  455.8 2.6 copy-start.2
  458.4 3.1 copy-start.1
Sparse Core Ops, SparseCore 0:
  75.2 207.9 reduce-scatter.3
  286.1 35.3 all-reduce.1
where the time goes:
time: 470 us; the launch traced here: 468 us
  waiting for transfers between devices  250 us (53%)
  local copies, waits for them, and re-layouts  90.3 us (19%)
  blocking collectives  64.1 us (14%)
  other arithmetic  26 us (6%)
  between operations  14.8 us (3%)
  matrix products  13.1 us (3%)
  starting transfers between devices  9.74 us (2%)
    unnamed x3, waiting for transfers between devices  188 us
    psum x1, blocking collectives, per_device(): stats = lax.psum(local_sums, ('rep', 'shard'))  41.9 us
    psum x1, waiting for transfers between devices, per_device(): grad = lax.psum(partial_value, 'rep').astype(jnp.float32)  36.1 us
    unnamed x16, local copies, waits for them, and re-layouts  34.2 us
    all_to_all x1, waiting for transfers between devices, per_device(): lax.all_to_all(rollout_blocks(new_master[None].astype(jnp.bfloat16)), 'sh...  25.9 us
    broadcast_in_dim x4, local copies, waits for them, and re-layouts, rollout_blocks(): by_rank = jnp.repeat(paired, TP // KV_HEADS, axis=2)  22.7 us
    psum x1, blocking collectives, per_device(): squares = lax.psum(jnp.sum(grad * grad), 'shard')  22.1 us
    unnamed x1, other arithmetic  15.4 us
  transfers between devices with their start and end apart: 4, of which 3 were waited for; matrix products, arithmetic and copies ran while one was open for 18% of the time, Pallas kernels for 0%

commit v1 on v0

v1 whole, which is shorter than its diff:
```python
import functools

import jax
import jax.numpy as jnp
from jax import lax
from jax.experimental import pallas as pl
from jax.experimental.pallas import tpu as pltpu
from jax.sharding import PartitionSpec as P

HEAD = 128
KV_HEADS = 4
TP = 8
SEQ_DEV = 4
WIDE = 2 * HEAD
LANES = 128
SUB = 16
TILE = 256
MESH = pl.DeviceIdType.MESH


def token_terms(seq_row, mask_row, new_row, old_row, ref_row):
    onehot = (seq_row[:, None] == jnp.arange(SEQ_DEV, dtype=jnp.int32)[None, :]).astype(jnp.float32)
    maskf = mask_row.astype(jnp.float32)
    lengths = jnp.maximum(jnp.sum(maskf[:, None] * onehot, axis=0), 1.0)
    tok_len = jnp.sum(onehot * lengths[None, :], axis=1)
    weight = maskf / tok_len
    ratio = -weight * jnp.exp(new_row - old_row)
    fixed = weight * (0.2 * (1.0 - jnp.exp(ref_row - new_row)))
    return jnp.concatenate(
        [onehot * ratio[:, None], fixed[:, None], jnp.zeros((onehot.shape[0], 3), jnp.float32)], axis=1
    )


def flip(index, bit):
    step = 1 << bit
    here = (index // step) % 2
    return index + (1 - 2 * here) * step, here


def exchange_kernel(
    n_rep, n_shard, split, group_ref, reward_ref, token_ref, hidden_ref, cot_ref, master_ref,
    mb_ref, gb_out, nm_out, scale_ref,
    part, sums, zin, grad, rows_in, delta, stage_in, stage_out,
    small, small_in, send_sems, recv_sems, local_sems,
):
    z_count = n_shard // 2
    rep_bits = n_rep.bit_length() - 1
    dims = rep_bits
    r, s = lax.axis_index("rep"), lax.axis_index("shard")
    core, x, zi = r % 2, s % 2, s // 2
    head = zi % KV_HEADS
    first = zi - head
    features, toks = hidden_ref.shape[1], hidden_ref.shape[0]
    layer_count, rows = master_ref.shape[0], master_ref.shape[1]
    sub = rows // split
    counter = [0]
    started = []

    def send(src, dst, device):
        number = counter[0]
        counter[0] += 1
        copy = pltpu.make_async_remote_copy(
            src_ref=src, dst_ref=dst, send_sem=send_sems.at[number], recv_sem=recv_sems.at[number],
            device_id=device, device_id_type=MESH,
        )
        copy.start()
        started.append(copy)
        return copy

    def local(src, dst, number):
        copy = pltpu.make_async_copy(src, dst, local_sems.at[number])
        copy.start()
        return copy

    mate = (flip(r, 0)[0], s)
    options = []
    for bit in range(1, rep_bits):
        other, here = flip(r, bit)
        options.append((other, s, here))
    other, here = flip(s, 0)
    options.append((r, other, here))
    partners, bits = [], []
    for i in range(dims):
        a, b = options[i], options[(i + 1) % dims]
        partners.append(tuple(a[k] + core * (b[k] - a[k]) for k in range(2)))
        bits.append(a[2] + core * (b[2] - a[2]))
    z_peers = [None] + [(r, ((zi + d) % z_count) * 2 + x) for d in range(1, z_count)]
    tp_zi = [first + (head + d) % KV_HEADS for d in range(KV_HEADS)]
    tp_peers = [(r, tp_zi[d] * 2 + x) for d in range(KV_HEADS)]

    quarter = r % split
    fetch = local(master_ref.at[:, pl.ds(pl.multiple_of(quarter * sub, SUB), sub), :], stage_in, 0)

    barrier = pltpu.get_barrier_semaphore()
    everyone = [mate] + [o[:2] for o in options] + z_peers[1:]
    for device in everyone:
        pl.semaphore_signal(barrier, inc=1, device_id=device, device_id_type=MESH)

    hot, reward = group_ref[...], reward_ref[...]
    small[0] = jnp.concatenate(
        [jnp.sum(hot, axis=0, keepdims=True), jnp.sum(hot * reward, axis=0, keepdims=True),
         jnp.sum(hot * (reward * reward), axis=0, keepdims=True),
         jnp.zeros((5, hot.shape[1]), jnp.float32)], axis=0)
    pl.semaphore_wait(barrier, len(everyone))

    stat_copies = [send(small.at[0], small_in.at[d - 1], z_peers[d]) for d in range(1, z_count)]

    fetch.wait()
    for h in range(KV_HEADS):
        for l in range(layer_count):
            stage_out[h, l, :, :HEAD] = stage_in[l, :, h * HEAD:(h + 1) * HEAD].astype(jnp.bfloat16)
            low = KV_HEADS * HEAD + h * HEAD
            stage_out[h, l, :, HEAD:] = stage_in[l, :, low:low + HEAD].astype(jnp.bfloat16)
    yi = quarter // 2
    for copy in stat_copies:
        copy.wait_recv()
    slot = z_count - 1
    total = small[0]
    for d in range(1, z_count):
        total = total + small_in[d - 1]
    small[1] = total
    level = 1
    for k, device in enumerate([mate] + partners):
        copy = send(small.at[level], small_in.at[slot], device)
        if k == 0:
            own_copy = local(stage_out.at[head], mb_ref.at[core, x, yi, zi], 1)
            m1 = [send(stage_out.at[(head + d) % KV_HEADS], mb_ref.at[core, x, yi, zi], z_peers[d])
                  for d in range(1, z_count)]
        copy.wait_recv()
        total = total + small_in[slot]
        slot += 1
        level += 1
        small[level] = total

    count = jnp.maximum(total[0:1], 1.0)
    mean = total[1:2] / count
    spread = jnp.maximum(jnp.sqrt(jnp.maximum(total[2:3] / count - mean * mean, 0.0)), 0.5)
    own_mean = jnp.sum(hot * mean, axis=1, keepdims=True)
    own_std = jnp.sum(hot * spread, axis=1, keepdims=True)
    own_std = jnp.where(own_std > 0.0, own_std, 1.0)
    advantage = (reward[:, 0:1] - own_mean) / own_std
    coef = token_ref[:, SEQ_DEV:SEQ_DEV + 1]
    for j in range(SEQ_DEV):
        coef = coef + token_ref[:, j:j + 1] * advantage[j:j + 1, :]
    for h in range(KV_HEADS):
        for side in range(2):
            low = side * KV_HEADS * HEAD + h * HEAD
            at = h * WIDE + side * HEAD
            delta[:, at:at + HEAD] = (coef * cot_ref[:, low:low + HEAD].astype(jnp.float32)).astype(jnp.bfloat16)

    half = features // 2

    def multiply(base):
        @pl.loop(0, half // TILE)
        def _(i):
            at = pl.multiple_of(base + i * TILE, TILE)
            out = lax.dot_general(
                hidden_ref[:, pl.ds(at, TILE)], delta[...], (((0,), (0,)), ((), ())),
                preferred_element_type=jnp.float32,
            ).astype(jnp.bfloat16)
            for h in range(KV_HEADS):
                part[h, pl.ds(at, TILE), :] = out[:, h * WIDE:(h + 1) * WIDE]

    offsets, lens = [core * half], [half]
    for i in range(dims):
        lens.append(lens[-1] // 2)
        offsets.append(offsets[-1] + bits[i] * lens[-1])
    starts, at = [], 0
    for length in lens:
        starts.append(at)
        at += length
    order = [(head + k + 1) % KV_HEADS for k in range(KV_HEADS)]

    away = (1 - core) * half
    multiply(away)
    inbound = {}
    for k in range(KV_HEADS):
        inbound[0, k] = send(
            part.at[order[k], pl.ds(pl.multiple_of(away, SUB), half)],
            sums.at[order[k], pl.ds(starts[0], half)], mate)
    multiply(core * half)

    own_copy.wait()
    for copy in m1:
        copy.wait_recv()
    xy = [(r, flip(s, 0)[0])]
    first_at = (1 - x, yi)
    if split == 4:
        other = flip(r, 1)[0]
        xy = [(r + core * (other - r), s + (1 - core) * (1 - 2 * x)),
              (r + (1 - core) * (other - r), s + core * (1 - 2 * x))]
        first_at = (x + (1 - core) * (1 - 2 * x), yi + core * (1 - 2 * yi))
    own_block = mb_ref.at[core, x, yi]
    spread_copies = [send(own_block, own_block, device) for device in xy]
    forward = []

    inner = min(lens[-1], 112)

    def add_in(i, h):
        base = offsets[i]

        @pl.loop(0, lens[i] // inner)
        def _(t):
            at = pl.multiple_of(base + t * inner, SUB)
            from_at = pl.multiple_of(starts[i] + t * inner, SUB)
            part[h, pl.ds(at, inner), :] = (
                part[h, pl.ds(at, inner), :].astype(jnp.float32)
                + sums[h, pl.ds(from_at, inner), :].astype(jnp.float32)
            ).astype(jnp.bfloat16)

    z_copies = []
    for t in range(KV_HEADS + dims):
        for i in range(dims + 1):
            k = t - i
            if k < 0 or k >= KV_HEADS:
                continue
            inbound[i, k].wait_recv()
            add_in(i, order[k])
            if i < dims:
                gone = offsets[i] + (1 - bits[i]) * lens[i + 1]
                inbound[i + 1, k] = send(
                    part.at[order[k], pl.ds(pl.multiple_of(gone, SUB), lens[i + 1])],
                    sums.at[order[k], pl.ds(starts[i + 1], lens[i + 1])], partners[i])
            else:
                for d in range(1, z_count):
                    if d % KV_HEADS == (k + 1) % KV_HEADS:
                        z_copies.append(send(
                            part.at[order[k], pl.ds(pl.multiple_of(offsets[-1], SUB), lens[-1])],
                            zin.at[d - 1], z_peers[d]))
        if t == 2 and split == 4:
            spread_copies[0].wait_recv()
            block = mb_ref.at[core, first_at[0], first_at[1]]
            forward.append(send(block, block, xy[1]))

    for copy in z_copies:
        copy.wait_recv()
    base = offsets[-1]

    def gather_sum(t, acc):
        at = pl.multiple_of(base + t * inner, SUB)
        g = part[head, pl.ds(at, inner), :].astype(jnp.float32)
        for d in range(1, z_count):
            g = g + zin[d - 1, pl.ds(pl.multiple_of(t * inner, SUB), inner), :].astype(jnp.float32)
        grad[pl.ds(at, inner), :] = g.astype(jnp.bfloat16)
        return acc + jnp.sum(g * g, axis=0, keepdims=True)

    squares = lax.fori_loop(0, lens[-1] // inner, gather_sum, jnp.zeros((1, WIDE), jnp.float32))
    square = jnp.broadcast_to(jnp.sum(squares, axis=1, keepdims=True), small.shape[1:])
    level += 1
    small[level] = square
    square_copies = []
    for d in range(1, KV_HEADS):
        square_copies.append(send(small.at[level], small_in.at[slot], tp_peers[d]))
        slot += 1
    slot_base = slot - (KV_HEADS - 1)

    for step, i in enumerate(list(reversed(range(dims))) + [-1]):
        device = mate if i < 0 else partners[i]
        span = pl.ds(pl.multiple_of(offsets[i + 1], SUB), lens[i + 1])
        copy = send(grad.at[span], grad.at[span], device)
        if step == 0:
            for other in square_copies:
                other.wait_recv()
            for d in range(KV_HEADS - 1):
                square = square + small_in[slot_base + d]
        level += 1
        small[level] = square
        square_copy = send(small.at[level], small_in.at[slot], device)
        square_copy.wait_recv()
        square = square + small_in[slot]
        slot += 1
        copy.wait_recv()

    piece = rows // 2
    nm_copies = []
    mine = pl.ds(pl.multiple_of(core * piece, SUB), piece)
    for d in range(1, KV_HEADS):
        at = pl.multiple_of((tp_zi[d] * 2 + x) * rows + core * piece, SUB)
        nm_copies.append(send(grad.at[pl.ds(at, piece)], rows_in.at[head, mine], tp_peers[d]))

    for copy in spread_copies[len(spread_copies) - 1:] + forward:
        copy.wait_recv()
    last = send(mb_ref.at[core], mb_ref.at[core], mate)

    rms = jnp.sqrt(square / (features * KV_HEADS * WIDE) + 1e-06)
    scale_ref[...] = 0.5 / rms[:, :LANES]
    done = [local(grad, gb_out, 0)]
    done.append(local(grad.at[pl.ds(pl.multiple_of(s * rows, SUB), rows)], nm_out.at[head], 1))
    passed = []
    for d in range(1, KV_HEADS):
        nm_copies[d - 1].wait_recv()
        source = (head + KV_HEADS - d) % KV_HEADS
        passed.append(send(rows_in.at[source, mine], rows_in.at[source, mine], mate))
    for d in range(1, KV_HEADS):
        passed[d - 1].wait_recv()
        source = (head + KV_HEADS - d) % KV_HEADS
        done.append(local(rows_in.at[source], nm_out.at[source], d + 1))
    last.wait_recv()
    for copy in done:
        copy.wait()
    for copy in started:
        copy.wait_send()


def finish_kernel(mb_ref, gb_ref, nm_ref, scale_ref, master_ref, new_ref, out_ref):
    scale = scale_ref[0:1, 0:1]
    for h in range(KV_HEADS):
        for side in range(2):
            low = side * KV_HEADS * HEAD + h * HEAD
            new_ref[:, low:low + HEAD] = (
                master_ref[0, :, low:low + HEAD]
                - scale * nm_ref[h, :, side * HEAD:(side + 1) * HEAD].astype(jnp.float32))
    _, _, y_count, z_count, layer_count, sub, _ = mb_ref.shape
    for z in range(z_count):
        for x in range(2):
            for y in range(y_count):
                for c in range(2):
                    at = (((z * 2 + x) * y_count + y) * 2 + c) * sub
                    span = slice(at, at + sub)
                    out_ref[0, span, :] = (
                        mb_ref[c, x, y, z, 0].astype(jnp.float32)
                        - scale * gb_ref[span, :].astype(jnp.float32)).astype(jnp.bfloat16)
                    for l in range(1, layer_count):
                        out_ref[l, span, :] = mb_ref[c, x, y, z, l]


def per_device(
    n_rep, n_shard, hidden, cotangent, seq_ids, response_mask, group_ids, rewards, new_logp, old_logp, ref_logp,
    master,
):
    groups = n_rep * n_shard * SEQ_DEV // 8
    wide = -(-groups // LANES) * LANES
    toks, features = hidden.shape
    layer_count, rows, cols = master.shape
    z_count = n_shard // 2
    split = 4 if n_rep % 4 == 0 and (rows // 4) % SUB == 0 else 2
    sub = rows // split
    dims = n_rep.bit_length() - 1
    final = features // 2 ** (dims + 1)
    hot = (group_ids[0][:, None] == jnp.arange(wide, dtype=jnp.int32)[None, :]).astype(jnp.float32)
    hot = jnp.pad(hot, ((0, 8 - SEQ_DEV), (0, 0)))
    reward = jnp.broadcast_to(jnp.pad(rewards[0], (0, 8 - SEQ_DEV))[:, None], (8, wide))
    terms = token_terms(seq_ids[0], response_mask[0], new_logp[0], old_logp[0], ref_logp[0])
    bf16, f32 = jnp.bfloat16, jnp.float32
    vmem, hbm = pl.BlockSpec(memory_space=pltpu.VMEM), pl.BlockSpec(memory_space=pl.ANY)
    mb_shape = (2, 2, split // 2, z_count, layer_count, sub, WIDE)
    sem_count = 64 + 4 * z_count
    landing = features // 2 * 2
    mb, gb, nm, scale = pl.pallas_call(
        functools.partial(exchange_kernel, n_rep, n_shard, split),
        out_shape=(
            jax.ShapeDtypeStruct(mb_shape, bf16),
            jax.ShapeDtypeStruct((features, WIDE), bf16),
            jax.ShapeDtypeStruct((KV_HEADS, rows, WIDE), bf16),
            jax.ShapeDtypeStruct((8, LANES), f32),
        ),
        in_specs=[vmem] * 5 + [hbm],
        out_specs=(hbm, hbm, hbm, vmem),
        scratch_shapes=[
            pltpu.VMEM((KV_HEADS, features, WIDE), bf16),
            pltpu.VMEM((KV_HEADS, landing, WIDE), bf16),
            pltpu.VMEM((z_count - 1, final, WIDE), bf16),
            pltpu.VMEM((features, WIDE), bf16),
            pltpu.VMEM((KV_HEADS, rows, WIDE), bf16),
            pltpu.VMEM((toks, cols), bf16),
            pltpu.VMEM((layer_count, sub, cols), f32),
            pltpu.VMEM((KV_HEADS, layer_count, sub, WIDE), bf16),
            pltpu.VMEM((2 * dims + 6, 8, wide), f32),
            pltpu.VMEM((z_count + 2 * dims + 6, 8, wide), f32),
            pltpu.SemaphoreType.DMA((sem_count,)),
            pltpu.SemaphoreType.DMA((sem_count,)),
            pltpu.SemaphoreType.DMA((8,)),
        ],
        compiler_params=pltpu.CompilerParams(
            collective_id=0, has_side_effects=True, vmem_limit_bytes=56 * 2**20
        ),
        name="exchange",
    )(hot, reward, terms, hidden, cotangent, master)
    steps = KV_HEADS
    new_master, rollout = pl.pallas_call(
        finish_kernel,
        grid=(steps,),
        out_shape=(
            jax.ShapeDtypeStruct((rows, cols), f32),
            jax.ShapeDtypeStruct((layer_count, features, WIDE), bf16),
        ),
        in_specs=[
            pl.BlockSpec((2, 2, split // 2, z_count // steps, layer_count, sub, WIDE),
                         lambda i: (0, 0, 0, i, 0, 0, 0)),
            pl.BlockSpec((features // steps, WIDE), lambda i: (i, 0)),
            pl.BlockSpec((KV_HEADS, rows // steps, WIDE), lambda i: (0, i, 0)),
            pl.BlockSpec((8, LANES), lambda i: (0, 0)),
            pl.BlockSpec((1, rows // steps, cols), lambda i: (0, i, 0)),
        ],
        out_specs=(
            pl.BlockSpec((rows // steps, cols), lambda i: (i, 0)),
            pl.BlockSpec((layer_count, features // steps, WIDE), lambda i: (0, i, 0)),
        ),
        name="finish",
    )(mb, gb, nm, scale, master)
    return (new_master, rollout)


def solution(mesh):
    tokens = P(("rep", "shard"), None)
    return jax.shard_map(
        functools.partial(per_device, mesh.shape["rep"], mesh.shape["shard"]),
        mesh=mesh,
        in_specs=(tokens,) * 9 + (P(None, "shard", None),),
        out_specs=(P("shard", None), P(None, None, "shard")),
        check_vma=False,
    )
```

time: 470 us -> 128 us (0.27)
  waiting for transfers between devices: 250 us -> 0 us
  Pallas kernels: 0 us -> 119 us
  local copies, waits for them, and re-layouts: 90.3 us -> 2.22 us
  blocking collectives: 64.1 us -> 0 us
  other arithmetic: 26 us -> 5.8 us
  between operations: 14.8 us -> 0.65 us
  matrix products: 13.1 us -> 0 us
  starting transfers between devices: 9.74 us -> 0 us
    unnamed x3 -> x0, waiting for transfers between devices: 188 us -> none
    pallas_call x0 -> x2, Pallas kernels: none -> 119 us  [the longest x1 112 us: per_device(): pl.pallas_call(functools.partial(exchange_kernel, n_rep, n_shard, split),...]
    psum x2 -> x0, blocking collectives: 64.1 us -> none  [the longest x1 41.9 us: per_device(): stats = lax.psum(local_sums, ('rep', 'shard'))]
    psum x1 -> x0, waiting for transfers between devices: 36.1 us -> none  [per_device(): grad = lax.psum(partial_value, 'rep').astype(jnp.float32)]
    unnamed x16 -> x0, local copies, waits for them, and re-layouts: 34.2 us -> none
    all_to_all x2 -> x0, waiting for transfers between devices: 25.9 us -> none  [the longest x1 25.9 us: per_device(): lax.all_to_all(rollout_blocks(new_master[None].astype(jnp.bfloat16)), 'sh...]
    broadcast_in_dim x4 -> x2, local copies, waits for them, and re-layouts: 22.7 us -> 0.66 us  [the longest x1 0.66 us: per_device(): jnp.broadcast_to(jnp.pad(rewards[0], (0, 8 - SEQ_DEV))[:, None], (8, wide))]
    all_to_all x3 -> x0, local copies, waits for them, and re-layouts: 16.1 us -> none  [the longest x1 11.1 us: per_device(): lax.all_to_all(rollout_blocks(master[1:].astype(jnp.bfloat16)), 'shard',...]
  transfers between devices with their start and end apart: 4 -> 0, of which waited for: 3 -> 0; matrix products, arithmetic and copies ran while one was open for 18% -> 0% of each run, Pallas kernels for 0% -> 0%
where the time goes in v1:
time: 128 us
  Pallas kernels  119 us (93%)
  other arithmetic  5.8 us (5%)
  local copies, waits for them, and re-layouts  2.22 us (2%)
    pallas_call x1, Pallas kernels, per_device(): pl.pallas_call(functools.partial(exchange_kernel, n_rep, n_shard, split),...  112 us
    pallas_call x1, Pallas kernels, per_device(): pl.pallas_call(finish_kernel, grid=(steps,), out_shape=(jax.ShapeDtypeStr...  6.91 us

profile of v1, /device:TPU:0, one launch (start us, length us, event | category | flops | bytes accessed | tf_op | source)
XLA Modules:
  0.0 128.0 jit_solution(3539817078143685820)
XLA Ops:
  0.6 0.7 iota_compare_fusion.1
  1.4 0.7 pad.12
  2.0 0.1 pad.15.clone
  2.1 0.7 subtract_exponential_fusion
  2.8 0.7 convert_element_type.28
  3.5 0.8 select_reduce_fusion.1
  4.3 0.8 select_reduce_fusion
  5.1 0.7 bitcast_multiply_fusion
  5.8 0.7 broadcast_in_dim.4.reward_ref
  6.5 0.6 pad_convert_fusion.group_ref
  7.1 0.7 fusion
  7.8 0.1 maximum_maximum_fusion
  7.8 0.8 copy.15.token_ref
  8.7 112.4 %exchange.1 = (bf16[2,2,2,4,3,112,256]{6,5,4,3,2,1,0:T(8,128)(2,1)}, bf16[3584,256]{1,0:T(8,128)(2,1)}, bf16[4,448,256]{2,1,0:T(8,128)(2,1)}, f32[8,128]{1,0:T(8,128)}) custom-call(f32[8,128]{1,0:T(8,128)} %pad_convert_fusion.group_ref, f32[8,128]{1,0:T(8,128)} %broadcast_in_dim.4.reward_ref, f32[448,8]{1,0:T(8,128)} %copy.15.token_ref, ...), custom_call_target="tpu_custom_call" | custom-call | tf_op jit(solution)/shard_map/exchange/pallas_call | solution.py:349
  121.1 6.9 %finish.1 = (f32[448,1024]{1,0:T(8,128)}, bf16[3,3584,256]{2,1,0:T(8,128)(2,1)}) custom-call(bf16[2,2,2,4,3,112,256]{6,5,4,3,2,1,0:T(8,128)(2,1)} %get-tuple-element.6.mb_ref, bf16[3584,256]{1,0:T(8,128)(2,1)} %get-tuple-element.7.gb_ref, bf16[4,448,256]{2,1,0:T(8,128)(2,1)} %get-tuple-element.8.nm_ref, f32[8,128]{1,0:T(8,128)} %get-tuple-element.9.scale_ref, ...), custom_call_target="tpu_custom_call" | custom-call | tf_op jit(solution)/shard_map/finish/pallas_call | solution.py:380
  (3 shorter events, 0.0 us)

commit v2 on v1

--- a/solution.py
+++ b/solution.py
@@ -18,17 +18,15 @@
 MESH = pl.DeviceIdType.MESH
 
 
-def token_terms(seq_row, mask_row, new_row, old_row, ref_row):
-    onehot = (seq_row[:, None] == jnp.arange(SEQ_DEV, dtype=jnp.int32)[None, :]).astype(jnp.float32)
+def token_rows(seq_row, mask_row, new_row, old_row, ref_row):
     maskf = mask_row.astype(jnp.float32)
-    lengths = jnp.maximum(jnp.sum(maskf[:, None] * onehot, axis=0), 1.0)
-    tok_len = jnp.sum(onehot * lengths[None, :], axis=1)
+    onehot = [(seq_row == j).astype(jnp.float32) for j in range(SEQ_DEV)]
+    tok_len = jnp.zeros_like(maskf)
+    for hot in onehot:
+        tok_len = tok_len + hot * jnp.maximum(jnp.sum(maskf * hot, axis=1, keepdims=True), 1.0)
     weight = maskf / tok_len
     ratio = -weight * jnp.exp(new_row - old_row)
-    fixed = weight * (0.2 * (1.0 - jnp.exp(ref_row - new_row)))
-    return jnp.concatenate(
-        [onehot * ratio[:, None], fixed[:, None], jnp.zeros((onehot.shape[0], 3), jnp.float32)], axis=1
-    )
+    return [hot * ratio for hot in onehot] + [weight * (0.2 * (1.0 - jnp.exp(ref_row - new_row)))]
 
 
 def flip(index, bit):
@@ -38,10 +36,11 @@
 
 
 def exchange_kernel(
-    n_rep, n_shard, split, group_ref, reward_ref, token_ref, hidden_ref, cot_ref, master_ref,
+    n_rep, n_shard, split, group_ref, reward_ref, seq_ref, mask_ref, new_ref, old_ref, ref_ref,
+    hidden_ref, cot_ref, master_ref,
     mb_ref, gb_out, nm_out, scale_ref,
     part, sums, zin, grad, rows_in, delta, stage_in, stage_out,
-    small, small_in, send_sems, recv_sems, local_sems,
+    small, small_in, token_t, send_sems, recv_sems, local_sems,
 ):
     z_count = n_shard // 2
     rep_bits = n_rep.bit_length() - 1
@@ -92,16 +91,32 @@
     fetch = local(master_ref.at[:, pl.ds(pl.multiple_of(quarter * sub, SUB), sub), :], stage_in, 0)
 
     barrier = pltpu.get_barrier_semaphore()
-    everyone = [mate] + [o[:2] for o in options] + z_peers[1:]
-    for device in everyone:
-        pl.semaphore_signal(barrier, inc=1, device_id=device, device_id_type=MESH)
-
-    hot, reward = group_ref[...], reward_ref[...]
+    everyone = n_rep * n_shard
+    me = r * n_shard + s
+
+    @pl.loop(1, everyone)
+    def _(i):
+        peer = (me + i) % everyone
+        pl.semaphore_signal(
+            barrier, inc=1, device_id=(peer // n_shard, peer % n_shard), device_id_type=MESH)
+
+    shape = small.shape[1:]
+    line = lax.broadcasted_iota(jnp.int32, shape, 0)
+    lane = lax.broadcasted_iota(jnp.int32, shape, 1)
+    hot, reward = jnp.zeros(shape, jnp.float32), jnp.zeros(shape, jnp.float32)
+    for j in range(SEQ_DEV):
+        hot = jnp.where((line == j) & (lane == group_ref[0, j]), 1.0, hot)
+        reward = jnp.where(line == j, reward_ref[0, j], reward)
     small[0] = jnp.concatenate(
         [jnp.sum(hot, axis=0, keepdims=True), jnp.sum(hot * reward, axis=0, keepdims=True),
          jnp.sum(hot * (reward * reward), axis=0, keepdims=True),
          jnp.zeros((5, hot.shape[1]), jnp.float32)], axis=0)
-    pl.semaphore_wait(barrier, len(everyone))
+    token_t[...] = jnp.zeros_like(token_t)
+    terms = token_rows(seq_ref[...], mask_ref[...], new_ref[...], old_ref[...], ref_ref[...])
+    for j, row in enumerate(terms):
+        token_t[j:j + 1, :toks] = row
+    tokens = jnp.transpose(token_t[...])[:toks]
+    pl.semaphore_wait(barrier, everyone - 1)
 
     stat_copies = [send(small.at[0], small_in.at[d - 1], z_peers[d]) for d in range(1, z_count)]
 
@@ -112,6 +127,26 @@
             low = KV_HEADS * HEAD + h * HEAD
             stage_out[h, l, :, HEAD:] = stage_in[l, :, low:low + HEAD].astype(jnp.bfloat16)
     yi = quarter // 2
+    xy = [(r, flip(s, 0)[0])]
+    first_at = (1 - x, yi)
+    if split == 4:
+        other = flip(r, 1)[0]
+        xy = [(r + core * (other - r), s + (1 - core) * (1 - 2 * x)),
+              (r + (1 - core) * (other - r), s + core * (1 - 2 * x))]
+        first_at = (x + (1 - core) * (1 - 2 * x), yi + core * (1 - 2 * yi))
+        second_at = (x + core * (1 - 2 * x), yi + (1 - core) * (1 - 2 * yi))
+        third_at = (1 - x, 1 - yi)
+    spread_copies = []
+
+    def spread_block(d):
+        for e in range(d, z_count if d == KV_HEADS - 1 else d + 1):
+            if e:
+                m1[e - 1].wait_recv()
+            else:
+                own_copy.wait()
+            block = mb_ref.at[core, x, yi, (zi + z_count - e) % z_count]
+            spread_copies.append([send(block, block, device) for device in xy])
+
     for copy in stat_copies:
         copy.wait_recv()
     slot = z_count - 1
@@ -126,6 +161,8 @@
             own_copy = local(stage_out.at[head], mb_ref.at[core, x, yi, zi], 1)
             m1 = [send(stage_out.at[(head + d) % KV_HEADS], mb_ref.at[core, x, yi, zi], z_peers[d])
                   for d in range(1, z_count)]
+        if k == 1:
+            spread_block(0)
         copy.wait_recv()
         total = total + small_in[slot]
         slot += 1
@@ -139,15 +176,16 @@
     own_std = jnp.sum(hot * spread, axis=1, keepdims=True)
     own_std = jnp.where(own_std > 0.0, own_std, 1.0)
     advantage = (reward[:, 0:1] - own_mean) / own_std
-    coef = token_ref[:, SEQ_DEV:SEQ_DEV + 1]
+    coef = tokens[:, SEQ_DEV:SEQ_DEV + 1]
     for j in range(SEQ_DEV):
-        coef = coef + token_ref[:, j:j + 1] * advantage[j:j + 1, :]
+        coef = coef + tokens[:, j:j + 1] * advantage[j:j + 1, :]
     for h in range(KV_HEADS):
         for side in range(2):
             low = side * KV_HEADS * HEAD + h * HEAD
             at = h * WIDE + side * HEAD
             delta[:, at:at + HEAD] = (coef * cot_ref[:, low:low + HEAD].astype(jnp.float32)).astype(jnp.bfloat16)
 
+    spread_block(1)
     half = features // 2
 
     def multiply(base):
@@ -178,20 +216,12 @@
         inbound[0, k] = send(
             part.at[order[k], pl.ds(pl.multiple_of(away, SUB), half)],
             sums.at[order[k], pl.ds(starts[0], half)], mate)
+    spread_block(2)
     multiply(core * half)
 
-    own_copy.wait()
-    for copy in m1:
-        copy.wait_recv()
-    xy = [(r, flip(s, 0)[0])]
-    first_at = (1 - x, yi)
-    if split == 4:
-        other = flip(r, 1)[0]
-        xy = [(r + core * (other - r), s + (1 - core) * (1 - 2 * x)),
-              (r + (1 - core) * (other - r), s + core * (1 - 2 * x))]
-        first_at = (x + (1 - core) * (1 - 2 * x), yi + core * (1 - 2 * yi))
+    spread_block(3)
     own_block = mb_ref.at[core, x, yi]
-    spread_copies = [send(own_block, own_block, device) for device in xy]
+    to_mate = [send(own_block, own_block, mate)]
     forward = []
 
     inner = min(lens[-1], 112)
@@ -227,10 +257,12 @@
                         z_copies.append(send(
                             part.at[order[k], pl.ds(pl.multiple_of(offsets[-1], SUB), lens[-1])],
                             zin.at[d - 1], z_peers[d]))
-        if t == 2 and split == 4:
-            spread_copies[0].wait_recv()
+        if t == 3 and split == 4:
+            for pair in spread_copies:
+                pair[0].wait_recv()
             block = mb_ref.at[core, first_at[0], first_at[1]]
             forward.append(send(block, block, xy[1]))
+            to_mate.append(send(block, block, mate))
 
     for copy in z_copies:
         copy.wait_recv()
@@ -246,6 +278,21 @@
 
     squares = lax.fori_loop(0, lens[-1] // inner, gather_sum, jnp.zeros((1, WIDE), jnp.float32))
     square = jnp.broadcast_to(jnp.sum(squares, axis=1, keepdims=True), small.shape[1:])
+    mine = pl.ds(pl.multiple_of(base, SUB), lens[-1])
+    s_dst, inside = base // rows, base % rows
+    pieces = rows // lens[-1]
+    nm_number = counter[0]
+    nm_in = nm_number + n_rep // 2
+    counter[0] = nm_in + KV_HEADS * pieces
+    nm_copies = [
+        pltpu.make_async_remote_copy(
+            src_ref=grad.at[mine], dst_ref=rows_in.at[head, pl.ds(pl.multiple_of(inside, SUB), lens[-1])],
+            send_sem=send_sems.at[nm_number + j],
+            recv_sem=recv_sems.at[nm_in + head * pieces + inside // lens[-1]],
+            device_id=(2 * j + core, s_dst), device_id_type=MESH)
+        for j in range(n_rep // 2)]
+    dst_zi = s_dst // 2
+    leaves = (dst_zi != zi) & (dst_zi // KV_HEADS == zi // KV_HEADS)
     level += 1
     small[level] = square
     square_copies = []
@@ -254,10 +301,18 @@
         slot += 1
     slot_base = slot - (KV_HEADS - 1)
 
+    first_span = pl.ds(pl.multiple_of(offsets[dims], SUB), lens[dims])
+    first_copy = send(grad.at[first_span], grad.at[first_span], partners[dims - 1])
+
+    @pl.when(leaves)
+    def _():
+        for copy in nm_copies:
+            copy.start()
+
     for step, i in enumerate(list(reversed(range(dims))) + [-1]):
         device = mate if i < 0 else partners[i]
         span = pl.ds(pl.multiple_of(offsets[i + 1], SUB), lens[i + 1])
-        copy = send(grad.at[span], grad.at[span], device)
+        copy = first_copy if step == 0 else send(grad.at[span], grad.at[span], device)
         if step == 0:
             for other in square_copies:
                 other.wait_recv()
@@ -271,31 +326,64 @@
         slot += 1
         copy.wait_recv()
 
-    piece = rows // 2
-    nm_copies = []
-    mine = pl.ds(pl.multiple_of(core * piece, SUB), piece)
-    for d in range(1, KV_HEADS):
-        at = pl.multiple_of((tp_zi[d] * 2 + x) * rows + core * piece, SUB)
-        nm_copies.append(send(grad.at[pl.ds(at, piece)], rows_in.at[head, mine], tp_peers[d]))
-
-    for copy in spread_copies[len(spread_copies) - 1:] + forward:
-        copy.wait_recv()
-    last = send(mb_ref.at[core], mb_ref.at[core], mate)
+    if split == 4:
+        for pair in spread_copies:
+            pair[1].wait_recv()
+        block = mb_ref.at[core, second_at[0], second_at[1]]
+        to_mate.append(send(block, block, mate))
+        forward[0].wait_recv()
+        block = mb_ref.at[core, third_at[0], third_at[1]]
+    else:
+        for pair in spread_copies:
+            pair[0].wait_recv()
+        block = mb_ref.at[core, first_at[0], first_at[1]]
+    to_mate.append(send(block, block, mate))
 
     rms = jnp.sqrt(square / (features * KV_HEADS * WIDE) + 1e-06)
     scale_ref[...] = 0.5 / rms[:, :LANES]
     done = [local(grad, gb_out, 0)]
     done.append(local(grad.at[pl.ds(pl.multiple_of(s * rows, SUB), rows)], nm_out.at[head], 1))
-    passed = []
-    for d in range(1, KV_HEADS):
-        nm_copies[d - 1].wait_recv()
-        source = (head + KV_HEADS - d) % KV_HEADS
-        passed.append(send(rows_in.at[source, mine], rows_in.at[source, mine], mate))
-    for d in range(1, KV_HEADS):
-        passed[d - 1].wait_recv()
-        source = (head + KV_HEADS - d) % KV_HEADS
-        done.append(local(rows_in.at[source], nm_out.at[source], d + 1))
-    last.wait_recv()
+    others = [(head + d) % KV_HEADS for d in range(1, KV_HEADS)]
+    pass_number = counter[0]
+    counter[0] += KV_HEADS - 1
+    passed = [
+        pltpu.make_async_remote_copy(
+            src_ref=rows_in.at[h], dst_ref=rows_in.at[h], send_sem=send_sems.at[pass_number + n],
+            recv_sem=recv_sems.at[pass_number + n], device_id=mate, device_id_type=MESH)
+        for n, h in enumerate(others)]
+    keeper = (s * rows) // half
+
+    @pl.when(core == keeper)
+    def _():
+        for n, h in enumerate(others):
+            for p in range(pieces):
+                pltpu.make_async_remote_copy(
+                    src_ref=rows_in.at[h, pl.ds(p * lens[-1], lens[-1])],
+                    dst_ref=rows_in.at[h, pl.ds(p * lens[-1], lens[-1])],
+                    send_sem=send_sems.at[nm_number], recv_sem=recv_sems.at[nm_in + h * pieces + p],
+                    device_id=mate, device_id_type=MESH).wait_recv()
+            passed[n].start()
+
+    @pl.when(core != keeper)
+    def _():
+        for copy in passed:
+            copy.wait_recv()
+
+    for n, h in enumerate(others):
+        done.append(local(rows_in.at[h], nm_out.at[h], n + 2))
+    for copy in to_mate:
+        copy.wait_recv()
+
+    @pl.when(core == keeper)
+    def _():
+        for copy in passed:
+            copy.wait_send()
+
+    @pl.when(leaves)
+    def _():
+        for copy in nm_copies:
+            copy.wait_send()
+
     for copy in done:
         copy.wait()
     for copy in started:
@@ -337,14 +425,11 @@
     sub = rows // split
     dims = n_rep.bit_length() - 1
     final = features // 2 ** (dims + 1)
-    hot = (group_ids[0][:, None] == jnp.arange(wide, dtype=jnp.int32)[None, :]).astype(jnp.float32)
-    hot = jnp.pad(hot, ((0, 8 - SEQ_DEV), (0, 0)))
-    reward = jnp.broadcast_to(jnp.pad(rewards[0], (0, 8 - SEQ_DEV))[:, None], (8, wide))
-    terms = token_terms(seq_ids[0], response_mask[0], new_logp[0], old_logp[0], ref_logp[0])
     bf16, f32 = jnp.bfloat16, jnp.float32
     vmem, hbm = pl.BlockSpec(memory_space=pltpu.VMEM), pl.BlockSpec(memory_space=pl.ANY)
+    smem = pl.BlockSpec(memory_space=pltpu.SMEM)
     mb_shape = (2, 2, split // 2, z_count, layer_count, sub, WIDE)
-    sem_count = 64 + 4 * z_count
+    sem_count = 64 + 8 * z_count
     landing = features // 2 * 2
     mb, gb, nm, scale = pl.pallas_call(
         functools.partial(exchange_kernel, n_rep, n_shard, split),
@@ -354,7 +439,7 @@
             jax.ShapeDtypeStruct((KV_HEADS, rows, WIDE), bf16),
             jax.ShapeDtypeStruct((8, LANES), f32),
         ),
-        in_specs=[vmem] * 5 + [hbm],
+        in_specs=[smem] * 2 + [vmem] * 7 + [hbm],
         out_specs=(hbm, hbm, hbm, vmem),
         scratch_shapes=[
             pltpu.VMEM((KV_HEADS, features, WIDE), bf16),
@@ -367,6 +452,7 @@
             pltpu.VMEM((KV_HEADS, layer_count, sub, WIDE), bf16),
             pltpu.VMEM((2 * dims + 6, 8, wide), f32),
             pltpu.VMEM((z_count + 2 * dims + 6, 8, wide), f32),
+            pltpu.VMEM((LANES, -(-toks // LANES) * LANES), f32),
             pltpu.SemaphoreType.DMA((sem_count,)),
             pltpu.SemaphoreType.DMA((sem_count,)),
             pltpu.SemaphoreType.DMA((8,)),
@@ -375,7 +461,7 @@
             collective_id=0, has_side_effects=True, vmem_limit_bytes=56 * 2**20
         ),
         name="exchange",
-    )(hot, reward, terms, hidden, cotangent, master)
+    )(group_ids, rewards, seq_ids, response_mask, new_logp, old_logp, ref_logp, hidden, cotangent, master)
     steps = KV_HEADS
     new_master, rollout = pl.pallas_call(
         finish_kernel,

time: 128 us -> 118 us (0.922)
  other arithmetic: 5.8 us -> 0 us
  local copies, waits for them, and re-layouts: 2.22 us -> 0 us
  Pallas kernels: 119 us -> 117 us
    pallas_call x1, Pallas kernels: 112 us -> 110 us  [per_device(): pl.pallas_call(functools.partial(exchange_kernel, n_rep, n_shard, split),...]
    reduce_sum x2 -> x0, other arithmetic: 1.57 us -> none  [the longest x1 0.8 us: token_terms(): lengths = jnp.maximum(jnp.sum(maskf[:, None] * onehot, axis=0), 1.0)]
    mul x3 -> x0, other arithmetic: 1.43 us -> none  [the longest x1 0.73 us: token_terms(): fixed = weight * (0.2 * (1.0 - jnp.exp(ref_row - new_row)))]
where the time goes in v2:
time: 118 us; the launch traced here: 117 us
  Pallas kernels  117 us (99%)
    pallas_call x1, Pallas kernels, per_device(): pl.pallas_call(functools.partial(exchange_kernel, n_rep, n_shard, split),...  110 us
    pallas_call x1, Pallas kernels, per_device(): pl.pallas_call(finish_kernel, grid=(steps,), out_shape=(jax.ShapeDtypeStr...  6.91 us

profile of v2, /device:TPU:0, one launch (start us, length us, event | category | flops | bytes accessed | tf_op | source)
XLA Modules:
  0.0 117.3 jit_solution(13009146937844125613)
XLA Ops:
  0.6 109.8 %exchange.1 = (bf16[2,2,2,4,3,112,256]{6,5,4,3,2,1,0:T(8,128)(2,1)}, bf16[3584,256]{1,0:T(8,128)(2,1)}, bf16[4,448,256]{2,1,0:T(8,128)(2,1)}, f32[8,128]{1,0:T(8,128)}) custom-call(s32[1,4]{1,0:T(1,128)} %group_ref.1, f32[1,4]{1,0:T(1,128)} %reward_ref.1, s32[1,448]{1,0:T(1,128)} %seq_ref.1, s32[1,448]{1,0:T(1,128)} %mask_ref.1, f32[1,448]{1,0:T(1,128)} %new_ref.1, ...), custom_call_target="tpu_custom_call" | custom-call | tf_op jit(solution)/shard_map/exchange/pallas_call | solution.py:434
  110.4 6.9 %finish.1 = (f32[448,1024]{1,0:T(8,128)}, bf16[3,3584,256]{2,1,0:T(8,128)(2,1)}) custom-call(bf16[2,2,2,4,3,112,256]{6,5,4,3,2,1,0:T(8,128)(2,1)} %get-tuple-element.6.mb_ref, bf16[3584,256]{1,0:T(8,128)(2,1)} %get-tuple-element.7.gb_ref, bf16[4,448,256]{2,1,0:T(8,128)(2,1)} %get-tuple-element.8.nm_ref, f32[8,128]{1,0:T(8,128)} %get-tuple-element.9.scale_ref, ...), custom_call_target="tpu_custom_call" | custom-call | tf_op jit(solution)/shard_map/finish/pallas_call | solution.py:466
